TPU v7x, 8 devices: a whole 2x2x1 slice. The times are simulated.
8 devices in a mesh: frag: 1 (over z), dev: 8 (over y, x, core).
Axes of the slice: x: 2, y: 2, z: 1, core: 2. Of those that a mesh axis runs over, the one named last changes fastest.
Arguments:
- a_ints: bfloat16 [144, 144, 144, 144], P(('frag', 'dev'))
- c_occ: bfloat16 [144, 24], P('frag')
- c_vir: bfloat16 [144, 120], P('frag')
- eps_occ: float32 [24], P('frag')
- eps_vir: float32 [120], P('frag')
Outputs:
- output: float32 [24, 24], P('frag', 'dev')
All inputs are finite; a program needn't handle non-finite values.
Results may differ from a plain program's by a relative error of at most 0.001.
Values are sent between devices in bfloat16 or wider.
A program may use at most 1 GiB of HBM per device.

v0:
```python
import jax
import jax.numpy as jnp
from jax import lax
from jax.sharding import PartitionSpec as P, NamedSharding


def pair_energies(v_mo, eps_j, eps_occ, eps_vir):
    v_swap = jnp.swapaxes(v_mo, 1, 2)
    denominator = (eps_j[:, None, None, None] + eps_occ[None, None, None, :]
                   - eps_vir[None, :, None, None] - eps_vir[None, None, :, None])
    pair_ji = jnp.sum(v_mo * (2.0 * v_mo - v_swap) / denominator, axis=(1, 2))
    return pair_ji.T


def solution(mesh):
    group_size = mesh.shape["dev"]

    def per_device(a_ints, c_occ, c_vir, eps_occ, eps_vir):
        occ_dev = c_occ.shape[1] // group_size
        t_one = jnp.einsum("pqrs,rj->pqsj", a_ints, c_occ, preferred_element_type=jnp.float32).astype(jnp.bfloat16)
        half_mo = jnp.einsum("pqsj,sb->pqjb", t_one, c_vir, preferred_element_type=jnp.float32).astype(jnp.bfloat16)
        half_mo = lax.all_to_all(half_mo, "dev", 2, 0, tiled=True)
        g_mat = jnp.einsum("pqjb,qa->pjba", half_mo, c_vir, preferred_element_type=jnp.float32).astype(jnp.bfloat16)
        v_mo = jnp.einsum("pjba,pi->jbai", g_mat, c_occ, preferred_element_type=jnp.float32)
        eps_j = lax.dynamic_slice_in_dim(eps_occ, lax.axis_index("dev") * occ_dev, occ_dev)
        return pair_energies(v_mo, eps_j, eps_occ, eps_vir)

    return jax.shard_map(
        per_device,
        mesh=mesh,
        in_specs=(P(("frag", "dev")), P("frag"), P("frag"), P("frag"), P("frag")),
        out_specs=P("frag", "dev"),
        check_vma=False,
    )
```

profile of v0, /device:TPU:0, one launch (start us, length us, event | category | flops | bytes accessed | tf_op | source)
XLA Modules:
  0.0 337.9 jit_solution(9138361738504694564)
XLA Ops:
  0.0 0.0 copy-start
  0.0 0.8 copy-done
  0.8 65.5 %fusion.8 = bf16[18,144,24,120]{3,2,1,0:T(8,128)(2,1)} fusion(bf16[18,144,144,144]{3,2,1,0:T(8,128)(2,1)} %param.5, bf16[144,120]{1,0:T(8,128)(2,1)S(1)} %copy-done, bf16[144,24]{0,1:T(8,128)(2,1)} %param.6), kind=kOutput, calls=%fused_computation.6 | convolution fusion | flops 4746221568 | bytes 122466816 | tf_op jit(solution)/shard_map/pqsj,sb->pqjb/dot_general | solution.py:21
  66.2 11.9 %copy.10 = bf16[18,144,24,120]{3,1,0,2:T(8,128)(2,1)} copy(bf16[18,144,24,120]{3,2,1,0:T(8,128)(2,1)} %fusion.8) | data formatting | bytes 29859840 | tf_op jit(solution)/shard_map/convert_element_type | solution.py:21
  78.1 0.0 copy-start.3
  78.1 0.0 copy-start.2
  78.1 4.5 %all-to-all-start = ((bf16[18,144,24,120]{3,1,0,2:T(8,128)(2,1)}), bf16[18,144,24,120]{3,1,0,2:T(8,128)(2,1)}, u32[]{:S(2)}, u32[]{:S(2)}) async-start(bf16[18,144,24,120]{3,1,0,2:T(8,128)(2,1)} %copy.10), calls=%async_computation | async-start | bytes 31850496 | tf_op jit(solution)/shard_map/all_to_all | solution.py:22
  82.6 0.0 copy-done.3
  82.7 0.1 dynamic_slice.3
  82.7 0.1 broadcast_add_fusion
  82.8 0.0 copy-done.2
  82.8 0.1 broadcast_subtract_fusion
  82.9 175.6 %all-to-all-done = bf16[18,144,24,120]{3,1,0,2:T(8,128)(2,1)} async-done(((bf16[18,144,24,120]{3,1,0,2:T(8,128)(2,1)}), bf16[18,144,24,120]{3,1,0,2:T(8,128)(2,1)}, u32[]{:S(2)}, u32[]{:S(2)}) %all-to-all-start) | async-done | bytes 14929952 | tf_op jit(solution)/shard_map/all_to_all | solution.py:22
  258.5 13.3 %copy.12 = bf16[8,18,144,3,120]{4,2,3,1,0:T(8,128)(2,1)} copy(bf16[8,18,144,3,120]{4,2,1,3,0:T(8,128)(2,1)} %bitcast.6) | data formatting | bytes 29859840 | tf_op jit(solution)/shard_map/all_to_all | solution.py:22
  271.8 0.0 copy-start.1
  271.8 38.6 %copy.13 = bf16[144,144,3,120]{1,0,3,2:T(8,128)(2,1)} copy(bf16[144,144,3,120]{3,1,2,0:T(8,128)(2,1)} %bitcast.36) | data formatting | bytes 29859840 | tf_op jit(solution)/shard_map/all_to_all | solution.py:22
  310.4 0.0 copy-done.1
  310.4 16.6 %fusion.4 = f32[3,120,120,24]{2,3,1,0:T(8,128)} fusion(bf16[144,144,3,120]{1,0,3,2:T(8,128)(2,1)} %copy.13, bf16[144,120]{1,0:T(8,128)(2,1)S(1)} %copy-done, bf16[144,24]{0,1:T(8,128)(2,1)S(1)} %copy-done.1), kind=kOutput, calls=%fused_computation.3 | convolution fusion | flops 2096409600 | bytes 19118592 | tf_op jit(solution)/shard_map/pjba,pi->jbai/dot_general | solution.py:24
  327.0 6.0 %copy.14 = f32[3,120,120,24]{1,3,2,0:T(8,128)} copy(f32[3,120,120,24]{2,3,1,0:T(8,128)} %fusion.4) | data formatting | bytes 8294400 | tf_op jit(solution)/shard_map/pjba,pi->jbai/dot_general | solution.py:24
  333.0 4.9 %fusion.13 = f32[3,24]{1,0:T(4,128)} fusion(f32[3,120,120,24]{2,3,1,0:T(8,128)} %fusion.4, f32[3,120,120,24]{1,3,2,0:T(8,128)} %copy.14, f32[120]{0:T(128)S(1)} %copy-done.2, f32[3,120,24]{2,1,0:T(8,128)S(1)} %broadcast_subtract_fusion), kind=kLoop, calls=%fused_computation.10 | loop fusion | flops 6220728 | bytes 8329728 | tf_op jit(solution)/shard_map/reduce_sum | solution.py:11
Async XLA Ops:
  0.0 0.8 copy-start
  78.1 4.5 %copy-start.3 = (f32[24]{0:T(128)S(1)}, f32[24]{0:T(128)}, u32[]{:S(2)}) copy-start(f32[24]{0:T(128)} %param.8) | copy-start | bytes 292
  78.1 4.7 %copy-start.2 = (f32[120]{0:T(128)S(1)}, f32[120]{0:T(128)}, u32[]{:S(2)}) copy-start(f32[120]{0:T(128)} %param.9) | copy-start | bytes 1444
  78.1 180.4 %all-to-all-start = ((bf16[18,144,24,120]{3,1,0,2:T(8,128)(2,1)}), bf16[18,144,24,120]{3,1,0,2:T(8,128)(2,1)}, u32[]{:S(2)}, u32[]{:S(2)}) async-start(bf16[18,144,24,120]{3,1,0,2:T(8,128)(2,1)} %copy.10), calls=%async_computation | async-start | bytes 31850496 | tf_op jit(solution)/shard_map/all_to_all | solution.py:22
  271.8 38.6 %copy-start.1 = (bf16[144,24]{0,1:T(8,128)(2,1)S(1)}, bf16[144,24]{0,1:T(8,128)(2,1)}, u32[]{:S(2)}) copy-start(bf16[144,24]{0,1:T(8,128)(2,1)} %param.6) | copy-start | bytes 20740
where the time goes:
time: 339 us; the launch traced here: 338 us
  waiting for transfers between devices  176 us (52%)
  matrix products  82 us (24%)
  local copies, waits for them, and re-layouts  70.6 us (21%)
  other arithmetic  5.1 us (2%)
  starting transfers between devices  4.52 us (1%)
    all_to_all x1, waiting for transfers between devices, per_device(): half_mo = lax.all_to_all(half_mo, 'dev', 2, 0, tiled=True)  176 us
    dot_general x1, matrix products, per_device(): jnp.einsum('pqsj,sb->pqjb', t_one, c_vir, preferred_element_type=jnp.floa...  65.5 us
    all_to_all x2, local copies, waits for them, and re-layouts, per_device(): half_mo = lax.all_to_all(half_mo, 'dev', 2, 0, tiled=True)  51.9 us
    dot_general x1, matrix products, per_device(): jnp.einsum('pjba,pi->jbai', g_mat, c_occ, preferred_element_type=jnp.floa...  16.6 us
    convert_element_type x1, local copies, waits for them, and re-layouts, per_device(): jnp.einsum('pqsj,sb->pqjb', t_one, c_vir, preferred_element_type=jnp.floa...  11.9 us
  transfers between devices with their start and end apart: 1, of which 1 were waited for; matrix products, arithmetic and copies ran while one was open for 0% of the time, Pallas kernels for 0%

commit v1 on v0

v1 whole, which is shorter than its diff:
```python
import functools

import jax
import jax.numpy as jnp
from jax import lax
from jax.experimental import pallas as pl
from jax.experimental.pallas import tpu as pltpu
from jax.sharding import PartitionSpec as P

MESH = pl.DeviceIdType.MESH
F32, BF16 = jnp.float32, jnp.bfloat16
NT = (((1,), (1,)), ((), ()))
LANES = 128
TILE = 16
QB = 16
SLOTS = 5


def iota(shape, dim):
    return lax.broadcasted_iota(jnp.int32, shape, dim)


def eye(n):
    return (iota((n, n), 0) == iota((n, n), 1)).astype(BF16)


def kernel(ndev, a_ref, co_ref, cv_ref, eo_ref, ev_ref, e_ref,
           abuf, t_scr, h_scr, g_scr, recv, v_scr, kron, cot, cvt, cvp, evrow, es,
           a_sem, send_sem, recv_sem):
    rows_p, n = a_ref.shape[0], a_ref.shape[1]
    o, v = co_ref.shape[1], cv_ref.shape[1]
    od = o // ndev
    pts = od * v
    nqb = n // QB
    nblk = rows_p * nqb
    me = lax.axis_index("dev")

    def partner(k):
        parts = [((me // s) % 2 + (k // s) % 2) % 2 * s for s in (4, 2, 1)]
        return parts[0] + parts[1] + parts[2]

    def fetch(blk):
        return pltpu.make_async_copy(
            a_ref.at[blk // nqb, pl.ds(blk % nqb * QB, QB)], abuf.at[blk % SLOTS], a_sem.at[blk % SLOTS])

    for s in range(SLOTS):
        fetch(s).start()

    barrier = pltpu.get_barrier_semaphore()
    for k in range(1, ndev):
        pl.semaphore_signal(barrier, inc=1, device_id={"dev": partner(k)}, device_id_type=MESH)

    cot[...] = lax.dot_general(eye(o), co_ref[...], NT, preferred_element_type=F32).astype(BF16)
    cvt[...] = lax.dot_general(eye(v), cv_ref[...], NT, preferred_element_type=F32).astype(BF16)
    cvp[...] = jnp.zeros_like(cvp)
    cvp[:, :v] = cv_ref[...]
    evrow[...] = jnp.ones_like(evrow)
    evrow[:, :v] = ev_ref[...]

    pl.semaphore_wait(barrier, ndev - 1)

    def send(k, p):
        return pltpu.make_async_remote_copy(
            src_ref=g_scr.at[p, partner(k)], dst_ref=recv.at[k - 1, p],
            send_sem=send_sem.at[k - 1, p], recv_sem=recv_sem.at[k - 1, p],
            device_id={"dev": partner(k)}, device_id_type=MESH)

    def row(p, _):
        def block(qb, _):
            blk = p * nqb + qb
            fetch(blk).wait()
            slot = blk % SLOTS
            for q in range(0, QB, 2):
                t = [jnp.dot(cot[...], abuf[slot, q + h], preferred_element_type=F32) for h in range(2)]
                t_scr[q * o:(q + 2) * o, :] = jnp.concatenate(t, 0).astype(BF16)
            h_scr[pl.ds(qb * QB * o, QB * o), :] = jnp.dot(t_scr[...], cvp[...], preferred_element_type=F32)

            @pl.when(blk + SLOTS < nblk)
            def _():
                fetch(blk + SLOTS).start()
            return 0

        lax.fori_loop(0, nqb, block, 0)
        for j in range(0, o, 2):
            h = jnp.concatenate([h_scr[pl.ds(j + x, n, stride=o), :] for x in range(2)], 1).astype(BF16)
            g = jnp.dot(cvt[...], h, preferred_element_type=F32).astype(BF16)
            for x in range(2):
                d, r = divmod(j + x, od)
                g_scr[p, d, r * v:(r + 1) * v, :] = g[:, x * LANES:(x + 1) * LANES]
        for k in (6, 7, 2, 3, 4, 5, 1):
            send(k, p).start()
        return 0

    lax.fori_loop(0, rows_p, row, 0)

    wide = 2 * ndev * TILE
    spread = (iota((o * TILE, o), 0) // TILE == iota((o * TILE, o), 1)).astype(BF16)
    cor = jnp.dot(spread, cot[...], preferred_element_type=F32).astype(BF16)
    col = iota((n, wide), 1) // TILE
    k = col // 2
    dev = ((me // 4 + k // 4) % 2) * 4 + ((me // 2 + k // 2) % 2) * 2 + (me + k) % 2
    src = dev * rows_p + col % 2
    keep = iota((o * TILE, wide), 0) % TILE == iota((o * TILE, wide), 1) % TILE
    for g in range(rows_p // 2):
        sel = (iota((n, wide), 0) == src + 2 * g).astype(BF16)
        m = jnp.dot(cor, sel, preferred_element_type=F32)
        kron[g] = jnp.where(keep, m, 0.0).astype(BF16)

    v_scr[...] = jnp.zeros_like(v_scr)

    def group(g, _):
        for s in range(1, ndev):
            for x in range(2):
                send(s, 2 * g + x).wait_recv()

        def rhs(r0):
            tiles = [g_scr[2 * g + x, me, pl.ds(r0, TILE), :] for x in range(2)]
            tiles += [recv[s, 2 * g + x, pl.ds(r0, TILE), :] for s in range(ndev - 1) for x in range(2)]
            return jnp.concatenate(tiles, 0)

        def pair(t, _):
            r0 = pl.multiple_of(t * 2 * TILE, 2 * TILE)
            out = jnp.dot(kron[g], jnp.concatenate([rhs(r0), rhs(r0 + TILE)], 1), preferred_element_type=F32)
            out = out.reshape(o, TILE, 2 * LANES)
            for x in range(2):
                v_scr[:, pl.ds(r0 + x * TILE, TILE), :] += out[:, :, x * LANES:(x + 1) * LANES]
            return 0

        full = pts // (2 * TILE)
        lax.fori_loop(0, full, pair, 0)
        rest = pts - full * 2 * TILE
        out = jnp.dot(kron[g], rhs(pts - TILE), preferred_element_type=F32).reshape(o, TILE, LANES)
        v_scr[:, pts - rest:pts, :] += out[:, TILE - rest:, :]
        return 0

    lax.fori_loop(0, rows_p // 2, group, 0)

    evb = jnp.broadcast_to(evrow[...], (LANES, LANES))
    evsum = (evb + evb.T)[:v]

    def energies(i, _):
        for j in range(od):
            x = v_scr[i, j * v:j * v + LANES, :]
            xt = x.T[:v]
            x = x[:v]
            e = x * (2.0 * x - xt) / (eo_ref[me * od + j] + eo_ref[i] - evsum)
            es[j, i] = jnp.sum(e.reshape(v // 8, 8, LANES), 0)
        return 0

    lax.fori_loop(0, o, energies, 0)
    for j in range(od):
        e_ref[:, j:j + 1] = jnp.sum(jnp.sum(es[j], 1), 1, keepdims=True)

    def drain(p, _):
        for s in range(1, ndev):
            send(s, p).wait_send()
        return 0

    lax.fori_loop(0, rows_p, drain, 0)


def solution(mesh):
    ndev = mesh.shape["dev"]

    def per_device(a_ints, c_occ, c_vir, eps_occ, eps_vir):
        rows_p, n = a_ints.shape[:2]
        o, v = c_occ.shape[1], c_vir.shape[1]
        od = o // ndev
        pts = od * v
        vm = pl.BlockSpec(memory_space=pltpu.VMEM)
        return pl.pallas_call(
            functools.partial(kernel, ndev),
            out_shape=jax.ShapeDtypeStruct((o, od), F32),
            in_specs=[pl.BlockSpec(memory_space=pl.ANY), vm, vm, pl.BlockSpec(memory_space=pltpu.SMEM), vm],
            out_specs=vm,
            scratch_shapes=[
                pltpu.VMEM((SLOTS, QB, n, n), BF16),
                pltpu.VMEM((QB * o, n), BF16),
                pltpu.VMEM((n * o, LANES), F32),
                pltpu.VMEM((rows_p, ndev, pts, LANES), BF16),
                pltpu.VMEM((ndev - 1, rows_p, pts, LANES), BF16),
                pltpu.VMEM((o, pts + 8, LANES), F32),
                pltpu.VMEM((rows_p // 2, o * TILE, 2 * ndev * TILE), BF16),
                pltpu.VMEM((o, n), BF16),
                pltpu.VMEM((v, n), BF16),
                pltpu.VMEM((n, LANES), BF16),
                pltpu.VMEM((1, LANES), F32),
                pltpu.VMEM((od, o, 8, LANES), F32),
                pltpu.SemaphoreType.DMA((SLOTS,)),
                pltpu.SemaphoreType.DMA((ndev - 1, rows_p)),
                pltpu.SemaphoreType.DMA((ndev - 1, rows_p)),
            ],
            compiler_params=pltpu.CompilerParams(
                collective_id=0, has_side_effects=True, vmem_limit_bytes=60 * 2**20),
        )(a_ints, c_occ, c_vir, eps_occ, eps_vir.reshape(1, v))

    return jax.shard_map(
        per_device,
        mesh=mesh,
        in_specs=(P(("frag", "dev")), P("frag"), P("frag"), P("frag"), P("frag")),
        out_specs=P("frag", "dev"),
        check_vma=False,
    )
```

time: 339 us -> 165 us (0.49)
  waiting for transfers between devices: 176 us -> 0 us
  Pallas kernels: 0 us -> 162 us
  matrix products: 82 us -> 0 us
  local copies, waits for them, and re-layouts: 70.6 us -> 2.77 us
  other arithmetic: 5.1 us -> 0 us
  starting transfers between devices: 4.52 us -> 0 us
    all_to_all x1 -> x0, waiting for transfers between devices: 176 us -> none  [per_device(): half_mo = lax.all_to_all(half_mo, 'dev', 2, 0, tiled=True)]
    pallas_call x0 -> x1, Pallas kernels: none -> 162 us  [per_device(): pl.pallas_call(functools.partial(kernel, ndev), out_shape=jax.ShapeDtypeS...]
    dot_general x2 -> x0, matrix products: 82 us -> none  [the longest x1 65.5 us: per_device(): jnp.einsum('pqsj,sb->pqjb', t_one, c_vir, preferred_element_type=jnp.floa...]
    all_to_all x2 -> x0, local copies, waits for them, and re-layouts: 51.9 us -> none  [per_device(): half_mo = lax.all_to_all(half_mo, 'dev', 2, 0, tiled=True)]
    convert_element_type x1 -> x0, local copies, waits for them, and re-layouts: 11.9 us -> none  [per_device(): jnp.einsum('pqsj,sb->pqjb', t_one, c_vir, preferred_element_type=jnp.floa...]
    dot_general x1 -> x0, local copies, waits for them, and re-layouts: 5.97 us -> none  [per_device(): jnp.einsum('pjba,pi->jbai', g_mat, c_occ, preferred_element_type=jnp.floa...]
    reduce_sum x1 -> x0, other arithmetic: 4.94 us -> none  [pair_energies(): pair_ji = jnp.sum(v_mo * (2.0 * v_mo - v_swap) / denominator, axis=(1, 2))]
    all_to_all x1 -> x0, starting transfers between devices: 4.52 us -> none  [per_device(): half_mo = lax.all_to_all(half_mo, 'dev', 2, 0, tiled=True)]
  transfers between devices with their start and end apart: 1 -> 0, of which waited for: 1 -> 0; matrix products, arithmetic and copies ran while one was open for 0% -> 0% of each run, Pallas kernels for 0% -> 0%
where the time goes in v1:
time: 165 us
  Pallas kernels  162 us (98%)
  local copies, waits for them, and re-layouts  2.77 us (2%)
    pallas_call x1, Pallas kernels, per_device(): pl.pallas_call(functools.partial(kernel, ndev), out_shape=jax.ShapeDtypeS...  162 us

profile of v1, /device:TPU:0, one launch (start us, length us, event | category | flops | bytes accessed | tf_op | source)
XLA Modules:
  0.0 164.8 jit_solution(15947145683898100782)
XLA Ops:
  0.0 1.4 copy.6.co_ref
  1.4 162.1 %shard_map.55 = f32[24,3]{1,0:T(8,128)} custom-call(bf16[18,144,144,144]{3,2,1,0:T(8,128)(2,1)} %a_ref.1, bf16[144,24]{1,0:T(8,128)(2,1)} %copy.6.co_ref, bf16[144,120]{1,0:T(8,128)(2,1)} %cv_ref.1, f32[24]{0:T(128)} %eo_ref.1, f32[1,120]{1,0:T(1,128)} %bitcast.1), custom_call_target="tpu_custom_call" | custom-call | tf_op jit(solution)/shard_map/pallas_call | solution.py:171
  163.5 1.4 copy.7

commit v2 on v1

v2 whole, which is shorter than its diff:
```python
import functools

import jax
import jax.numpy as jnp
from jax import lax
from jax.experimental import pallas as pl
from jax.experimental.pallas import tpu as pltpu
from jax.sharding import PartitionSpec as P

MESH = pl.DeviceIdType.MESH
F32, BF16 = jnp.float32, jnp.bfloat16
NT = (((1,), (1,)), ((), ()))
LANES = 128
TILE = 16
QB = 16
CHUNKS = 3
IC = 4
CUT = 176
PG = 4


def iota(shape, dim):
    return lax.broadcasted_iota(jnp.int32, shape, dim)


def eye(n):
    return (iota((n, n), 0) == iota((n, n), 1)).astype(BF16)


def kernel(ndev, a_ref, co_ref, cv_ref, eo_ref, ev_ref, e_ref,
           abuf, t_scr, h_scr, g_scr, recv_a, recv_b, v_own, v_rel, v_in, kron, kron_last, cot, cvt, cvp, evrow, es,
           a_sem, send_sem, recv_sem, vsend_sem, vrecv_sem):
    rows_p, n = a_ref.shape[0], a_ref.shape[1]
    o, v = co_ref.shape[1], cv_ref.shape[1]
    od = o // ndev
    pts = od * v
    nqb = n // QB
    me = lax.axis_index("dev")
    recv = (recv_a, recv_b)
    cut = recv_a.shape[3]
    base = (0, cut)
    size = (cut, pts - cut)
    first = (2, 4)
    second = (4, 2)

    def partner(k):
        parts = [((me // s) % 2 + (k // s) % 2) % 2 * s for s in (4, 2, 1)]
        return parts[0] + parts[1] + parts[2]

    def slots(h):
        return (0, 1, first[h], first[h] + 1)

    def fetch(p, x):
        return pltpu.make_async_copy(a_ref.at[p, pl.ds(x * QB, QB)], abuf.at[x], a_sem.at[x])

    for x in range(nqb):
        fetch(0, x).start()

    barrier = pltpu.get_barrier_semaphore()
    for k in range(1, 6):
        pl.semaphore_signal(barrier, inc=1, device_id={"dev": partner(k)}, device_id_type=MESH)

    cot[...] = lax.dot_general(eye(o), co_ref[...], NT, preferred_element_type=F32).astype(BF16)
    cvt[...] = lax.dot_general(eye(v), cv_ref[...], NT, preferred_element_type=F32).astype(BF16)
    cvp[...] = jnp.zeros_like(cvp)
    cvp[:, :v] = cv_ref[...]
    evrow[...] = jnp.ones_like(evrow)
    evrow[:, :v] = ev_ref[...]

    pl.semaphore_wait(barrier, 5)

    def send(h, s, t, p):
        k = slots(h)[s]
        return pltpu.make_async_remote_copy(
            src_ref=g_scr.at[p, partner(k ^ (t * second[h])), pl.ds(base[h], size[h])],
            dst_ref=recv[h].at[s - 1, p, t],
            send_sem=send_sem.at[h, s - 1, t, p], recv_sem=recv_sem.at[h, s - 1, t, p],
            device_id={"dev": partner(k)}, device_id_type=MESH)

    def send_sum(h, c):
        part = (pl.ds(c * IC, IC), pl.ds(base[h], size[h]))
        return pltpu.make_async_remote_copy(
            src_ref=v_rel.at[part], dst_ref=v_in.at[part],
            send_sem=vsend_sem.at[h, c], recv_sem=vrecv_sem.at[h, c],
            device_id={"dev": partner(second[h])}, device_id_type=MESH)

    def make_kron():
        spread = (iota((o * TILE, o), 0) // TILE == iota((o * TILE, o), 1)).astype(BF16)
        cor = jnp.dot(spread, cot[...], preferred_element_type=F32).astype(BF16)
        for h in range(2):
            def left(p0, np_):
                wide = 4 * np_ * TILE
                col = iota((n, wide), 1) // TILE
                slot = col // np_
                k = slot // 2 * first[h] + slot % 2
                dev = ((me // 4 + k // 4) % 2) * 4 + ((me // 2 + k // 2) % 2) * 2 + (me + k) % 2
                sel = (iota((n, wide), 0) == dev * rows_p + col % np_ + p0).astype(BF16)
                m = jnp.dot(cor, sel, preferred_element_type=F32)
                keep = iota((o * TILE, wide), 0) % TILE == iota((o * TILE, wide), 1) % TILE
                return jnp.where(keep, m, 0.0).astype(BF16)

            def full(g, _):
                kron[h, g] = left(g * PG, PG)
                return 0

            lax.fori_loop(0, rows_p // PG, full, 0)
            kron_last[h] = left(rows_p // PG * PG, rows_p % PG)

    def group(g, p0, np_):
        for h in range(2):
            def arrived(x, _):
                for s in range(1, 4):
                    for t in (1, 0):
                        send(h, s, t, p0 + x).wait_recv()
                return 0

            lax.fori_loop(0, np_, arrived, 0)

            def rhs(t, r0):
                tiles = [g_scr[pl.ds(p0, np_), partner(t * second[h]), pl.ds(base[h] + r0, TILE), :]]
                tiles += [recv[h][s, pl.ds(p0, np_), t, pl.ds(r0, TILE), :] for s in range(3)]
                return jnp.concatenate(tiles, 0).reshape(4 * np_ * TILE, LANES)

            def tile(r0, skip):
                left = kron[h, g] if np_ == PG else kron_last[h]
                out = jnp.dot(left, jnp.concatenate([rhs(0, r0), rhs(1, r0)], 1), preferred_element_type=F32)
                out = out.reshape(o, TILE, 2 * LANES)[:, skip:]
                at = pl.ds(base[h] + r0 + skip, TILE - skip)
                v_own[:, at, :] += out[:, :, :LANES]
                v_rel[:, at, :] += out[:, :, LANES:]

            def step(i, _):
                tile(pl.multiple_of(i * TILE, TILE), 0)
                return 0

            lax.fori_loop(0, size[h] // TILE, step, 0)
            if size[h] % TILE:
                tile(size[h] - TILE, TILE - size[h] % TILE)

    def row(p, _):
        rows_c = n // CHUNKS * o

        def second_step(c):
            h_scr[c * rows_c:(c + 1) * rows_c, :] = jnp.dot(t_scr[c % 2], cvp[...], preferred_element_type=F32)

        for c in range(CHUNKS):
            mine = range(c * nqb // CHUNKS, (c + 1) * nqb // CHUNKS)
            for x in mine:
                fetch(p, x).wait()
            pairs = len(mine) * QB // 2

            def first_step(i, _):
                q = c * pairs + i
                blk, r = q // (QB // 2), q % (QB // 2) * 2
                t = [jnp.dot(cot[...], abuf[blk, r + h], preferred_element_type=F32) for h in range(2)]
                at = pl.multiple_of(i * 2 * o, 2 * o)
                t_scr[c % 2, pl.ds(at, 2 * o), :] = jnp.concatenate(t, 0).astype(BF16)
                return 0

            lax.fori_loop(0, pairs, first_step, 0, unroll=True)
            if c:
                second_step(c - 1)
            for x in mine:
                fetch((p + 1) % rows_p, x).start()
        second_step(CHUNKS - 1)
        for j in range(0, o, 2):
            h = jnp.concatenate([h_scr[pl.ds(j + x, n, stride=o), :] for x in range(2)], 1).astype(BF16)
            g = jnp.dot(cvt[...], h, preferred_element_type=F32).astype(BF16)
            for x in range(2):
                d, r = divmod(j + x, od)
                g_scr[p, d, r * v:(r + 1) * v, :] = g[:, x * LANES:(x + 1) * LANES]
        for t in (1, 0):
            for s in (2, 3, 1):
                for h in range(2):
                    send(h, s, t, p).start()

        @pl.when(p == 0)
        def _():
            make_kron()
            v_own[...] = jnp.zeros_like(v_own)
            v_rel[...] = jnp.zeros_like(v_rel)

        @pl.when((p % PG == PG - 1) & (p > PG))
        def _():
            group(p // PG - 1, (p // PG - 1) * PG, PG)
        return 0

    lax.fori_loop(0, rows_p, row, 0)
    groups = rows_p // PG
    group(groups - 1, (groups - 1) * PG, PG)
    group(groups, groups * PG, rows_p % PG)
    def start_sum(c, _):
        for h in range(2):
            send_sum(h, c).start()
        return 0

    lax.fori_loop(0, o // IC, start_sum, 0)

    v_in[:, pts:, :] = jnp.zeros_like(v_in[:, pts:, :])
    evb = jnp.broadcast_to(evrow[...], (LANES, LANES))
    evsum = (evb + evb.T)[:v]

    def energies(c, _):
        for h in range(2):
            send_sum(h, c).wait_recv()

        def one(x, _):
            i = c * IC + x
            for j in range(od):
                at = pl.ds(j * v, LANES)
                x = v_own[i, at, :] + v_in[i, at, :]
                xt = x.T[:v]
                x = x[:v]
                e = x * (2.0 * x - xt) / (eo_ref[me * od + j] + eo_ref[i] - evsum)
                es[j, i] = jnp.sum(e.reshape(v // 8, 8, LANES), 0)
            return 0

        lax.fori_loop(0, IC, one, 0)
        return 0

    lax.fori_loop(0, o // IC, energies, 0)
    for j in range(od):
        e_ref[:, j:j + 1] = jnp.sum(jnp.sum(es[j], 1), 1, keepdims=True)

    for x in range(nqb):
        fetch(0, x).wait()

    def drain(p, _):
        for h in range(2):
            for s in range(1, 4):
                for t in range(2):
                    send(h, s, t, p).wait_send()
        return 0

    lax.fori_loop(0, rows_p, drain, 0)
    for c in range(o // IC):
        for h in range(2):
            send_sum(h, c).wait_send()


def solution(mesh):
    ndev = mesh.shape["dev"]

    def per_device(a_ints, c_occ, c_vir, eps_occ, eps_vir):
        rows_p, n = a_ints.shape[:2]
        o, v = c_occ.shape[1], c_vir.shape[1]
        od = o // ndev
        pts = od * v
        vm = pl.BlockSpec(memory_space=pltpu.VMEM)
        return pl.pallas_call(
            functools.partial(kernel, ndev),
            out_shape=jax.ShapeDtypeStruct((o, od), F32),
            in_specs=[pl.BlockSpec(memory_space=pl.ANY), vm, vm, pl.BlockSpec(memory_space=pltpu.SMEM), vm],
            out_specs=vm,
            scratch_shapes=[
                pltpu.VMEM((n // QB, QB, n, n), BF16),
                pltpu.VMEM((2, n // CHUNKS * o, n), BF16),
                pltpu.VMEM((n * o, LANES), F32),
                pltpu.VMEM((rows_p, ndev, pts, LANES), BF16),
                pltpu.VMEM((3, rows_p, 2, CUT, LANES), BF16),
                pltpu.VMEM((3, rows_p, 2, pts - CUT, LANES), BF16),
                pltpu.VMEM((o, pts + 8, LANES), F32),
                pltpu.VMEM((o, pts, LANES), F32),
                pltpu.VMEM((o, pts + 8, LANES), F32),
                pltpu.VMEM((2, 4, o * TILE, 16 * TILE), BF16),
                pltpu.VMEM((2, o * TILE, 8 * TILE), BF16),
                pltpu.VMEM((o, n), BF16),
                pltpu.VMEM((v, n), BF16),
                pltpu.VMEM((n, LANES), BF16),
                pltpu.VMEM((1, LANES), F32),
                pltpu.VMEM((od, o, 8, LANES), F32),
                pltpu.SemaphoreType.DMA((n // QB,)),
                pltpu.SemaphoreType.DMA((2, 3, 2, rows_p)),
                pltpu.SemaphoreType.DMA((2, 3, 2, rows_p)),
                pltpu.SemaphoreType.DMA((2, o // IC)),
                pltpu.SemaphoreType.DMA((2, o // IC)),
            ],
            compiler_params=pltpu.CompilerParams(
                collective_id=0, has_side_effects=True, vmem_limit_bytes=62 * 2**20),
        )(a_ints, c_occ, c_vir, eps_occ, eps_vir.reshape(1, v))

    return jax.shard_map(
        per_device,
        mesh=mesh,
        in_specs=(P(("frag", "dev")), P("frag"), P("frag"), P("frag"), P("frag")),
        out_specs=P("frag", "dev"),
        check_vma=False,
    )
```

time: 165 us -> 149 us (0.903)
  Pallas kernels: 162 us -> 145 us
    pallas_call x1, Pallas kernels: 162 us -> 145 us  [per_device(): pl.pallas_call(functools.partial(kernel, ndev), out_shape=jax.ShapeDtypeS...]
where the time goes in v2:
time: 149 us; the launch traced here: 148 us
  Pallas kernels  145 us (97%)
  local copies, waits for them, and re-layouts  2.77 us (2%)
    pallas_call x1, Pallas kernels, per_device(): pl.pallas_call(functools.partial(kernel, ndev), out_shape=jax.ShapeDtypeS...  145 us

profile of v2, /device:TPU:0, one launch (start us, length us, event | category | flops | bytes accessed | tf_op | source)
XLA Modules:
  0.0 148.3 jit_solution(1719597007833340881)
XLA Ops:
  0.0 1.4 copy.6.co_ref
  1.4 145.5 %shard_map.55 = f32[24,3]{1,0:T(8,128)} custom-call(bf16[18,144,144,144]{3,2,1,0:T(8,128)(2,1)} %a_ref.1, bf16[144,24]{1,0:T(8,128)(2,1)} %copy.6.co_ref, bf16[144,120]{1,0:T(8,128)(2,1)} %cv_ref.1, f32[24]{0:T(128)} %eo_ref.1, f32[1,120]{1,0:T(1,128)} %bitcast.1), custom_call_target="tpu_custom_call" | custom-call | tf_op jit(solution)/shard_map/pallas_call | solution.py:250
  146.9 1.4 copy.7

commit v3 on v2

--- a/solution.py
+++ b/solution.py
@@ -17,6 +17,7 @@
 IC = 4
 CUT = 176
 PG = 4
+DEFER = 15
 
 
 def iota(shape, dim):
@@ -28,7 +29,7 @@
 
 
 def kernel(ndev, a_ref, co_ref, cv_ref, eo_ref, ev_ref, e_ref,
-           abuf, t_scr, h_scr, g_scr, recv_a, recv_b, v_own, v_rel, v_in, kron, kron_last, cot, cvt, cvp, evrow, es,
+           abuf, t_scr, h_scr, g_scr, recv_a, recv_b, v_sum, v_in, kron, kron_last, cot, cvt, cvp, evrow, es,
            a_sem, send_sem, recv_sem, vsend_sem, vrecv_sem):
     rows_p, n = a_ref.shape[0], a_ref.shape[1]
     o, v = co_ref.shape[1], cv_ref.shape[1]
@@ -80,7 +81,7 @@
     def send_sum(h, c):
         part = (pl.ds(c * IC, IC), pl.ds(base[h], size[h]))
         return pltpu.make_async_remote_copy(
-            src_ref=v_rel.at[part], dst_ref=v_in.at[part],
+            src_ref=v_sum.at[(1,) + part], dst_ref=v_in.at[part],
             send_sem=vsend_sem.at[h, c], recv_sem=vrecv_sem.at[h, c],
             device_id={"dev": partner(second[h])}, device_id_type=MESH)
 
@@ -106,36 +107,47 @@
             lax.fori_loop(0, rows_p // PG, full, 0)
             kron_last[h] = left(rows_p // PG * PG, rows_p % PG)
 
-    def group(g, p0, np_):
+    def group(t, g, p0, np_):
         for h in range(2):
             def arrived(x, _):
                 for s in range(1, 4):
-                    for t in (1, 0):
-                        send(h, s, t, p0 + x).wait_recv()
+                    send(h, s, t, p0 + x).wait_recv()
                 return 0
 
             lax.fori_loop(0, np_, arrived, 0)
 
-            def rhs(t, r0):
+            def rhs(r0):
                 tiles = [g_scr[pl.ds(p0, np_), partner(t * second[h]), pl.ds(base[h] + r0, TILE), :]]
                 tiles += [recv[h][s, pl.ds(p0, np_), t, pl.ds(r0, TILE), :] for s in range(3)]
                 return jnp.concatenate(tiles, 0).reshape(4 * np_ * TILE, LANES)
 
-            def tile(r0, skip):
+            def tiles(*where):
                 left = kron[h, g] if np_ == PG else kron_last[h]
-                out = jnp.dot(left, jnp.concatenate([rhs(0, r0), rhs(1, r0)], 1), preferred_element_type=F32)
-                out = out.reshape(o, TILE, 2 * LANES)[:, skip:]
-                at = pl.ds(base[h] + r0 + skip, TILE - skip)
-                v_own[:, at, :] += out[:, :, :LANES]
-                v_rel[:, at, :] += out[:, :, LANES:]
+                right = [rhs(r0) for r0, _ in where]
+                out = jnp.dot(left, jnp.concatenate(right, 1), preferred_element_type=F32)
+                out = out.reshape(o, TILE, len(where) * LANES)
+                for x, (r0, skip) in enumerate(where):
+                    at = pl.ds(base[h] + r0 + skip, TILE - skip)
+                    v_sum[t, :, at, :] += out[:, skip:, x * LANES:(x + 1) * LANES]
 
             def step(i, _):
-                tile(pl.multiple_of(i * TILE, TILE), 0)
-                return 0
-
-            lax.fori_loop(0, size[h] // TILE, step, 0)
+                r0 = pl.multiple_of(i * 2 * TILE, 2 * TILE)
+                tiles((r0, 0), (r0 + TILE, 0))
+                return 0
+
+            pairs = size[h] // (2 * TILE)
+            lax.fori_loop(0, pairs, step, 0, unroll=True)
+            rest = [(r0, 0) for r0 in range(pairs * 2 * TILE, size[h] - TILE + 1, TILE)]
             if size[h] % TILE:
-                tile(size[h] - TILE, TILE - size[h] % TILE)
+                rest.append((size[h] - TILE, TILE - size[h] % TILE))
+            if rest:
+                tiles(*rest)
+
+    def late(p, _):
+        for s in (2, 3, 1):
+            for h in range(2):
+                send(h, s, 0, p).start()
+        return 0
 
     def row(p, _):
         rows_c = n // CHUNKS * o
@@ -169,32 +181,49 @@
             for x in range(2):
                 d, r = divmod(j + x, od)
                 g_scr[p, d, r * v:(r + 1) * v, :] = g[:, x * LANES:(x + 1) * LANES]
-        for t in (1, 0):
-            for s in (2, 3, 1):
-                for h in range(2):
-                    send(h, s, t, p).start()
+        for s in (2, 3, 1):
+            for h in range(2):
+                send(h, s, 1, p).start()
+
+        @pl.when(p < DEFER)
+        def _():
+            late(p, 0)
 
         @pl.when(p == 0)
         def _():
             make_kron()
-            v_own[...] = jnp.zeros_like(v_own)
-            v_rel[...] = jnp.zeros_like(v_rel)
+            v_sum[...] = jnp.zeros_like(v_sum)
 
         @pl.when((p % PG == PG - 1) & (p > PG))
         def _():
-            group(p // PG - 1, (p // PG - 1) * PG, PG)
+            g = p // PG - 1
+
+            def target(t, _):
+                group(t, g, g * PG, PG)
+                return 0
+
+            lax.fori_loop(0, 2, target, 0)
         return 0
 
     lax.fori_loop(0, rows_p, row, 0)
+    lax.fori_loop(DEFER, rows_p, late, 0)
     groups = rows_p // PG
-    group(groups - 1, (groups - 1) * PG, PG)
-    group(groups, groups * PG, rows_p % PG)
-    def start_sum(c, _):
-        for h in range(2):
-            send_sum(h, c).start()
-        return 0
-
-    lax.fori_loop(0, o // IC, start_sum, 0)
+
+    def finish(u, _):
+        group(1 - u, groups - 1, (groups - 1) * PG, PG)
+        group(1 - u, groups, groups * PG, rows_p % PG)
+
+        @pl.when(u == 0)
+        def _():
+            def start_sum(c, _):
+                for h in range(2):
+                    send_sum(h, c).start()
+                return 0
+
+            lax.fori_loop(0, o // IC, start_sum, 0)
+        return 0
+
+    lax.fori_loop(0, 2, finish, 0)
 
     v_in[:, pts:, :] = jnp.zeros_like(v_in[:, pts:, :])
     evb = jnp.broadcast_to(evrow[...], (LANES, LANES))
@@ -208,7 +237,7 @@
             i = c * IC + x
             for j in range(od):
                 at = pl.ds(j * v, LANES)
-                x = v_own[i, at, :] + v_in[i, at, :]
+                x = v_sum[0, i, at, :] + v_in[i, at, :]
                 xt = x.T[:v]
                 x = x[:v]
                 e = x * (2.0 * x - xt) / (eo_ref[me * od + j] + eo_ref[i] - evsum)
@@ -259,8 +288,7 @@
                 pltpu.VMEM((rows_p, ndev, pts, LANES), BF16),
                 pltpu.VMEM((3, rows_p, 2, CUT, LANES), BF16),
                 pltpu.VMEM((3, rows_p, 2, pts - CUT, LANES), BF16),
-                pltpu.VMEM((o, pts + 8, LANES), F32),
-                pltpu.VMEM((o, pts, LANES), F32),
+                pltpu.VMEM((2, o, pts + 8, LANES), F32),
                 pltpu.VMEM((o, pts + 8, LANES), F32),
                 pltpu.VMEM((2, 4, o * TILE, 16 * TILE), BF16),
                 pltpu.VMEM((2, o * TILE, 8 * TILE), BF16),

time: 149 us -> 140 us (0.940)
  Pallas kernels: 145 us -> 137 us
    pallas_call x1, Pallas kernels: 145 us -> 137 us  [per_device(): pl.pallas_call(functools.partial(kernel, ndev), out_shape=jax.ShapeDtypeS...]
where the time goes in v3:
time: 140 us
  Pallas kernels  137 us (98%)
  local copies, waits for them, and re-layouts  2.77 us (2%)
    pallas_call x1, Pallas kernels, per_device(): pl.pallas_call(functools.partial(kernel, ndev), out_shape=jax.ShapeDtypeS...  137 us

profile of v3, /device:TPU:0, one launch (start us, length us, event | category | flops | bytes accessed | tf_op | source)
XLA Modules:
  0.0 140.0 jit_solution(2064639784642449546)
XLA Ops:
  0.0 1.4 %copy.6.co_ref = bf16[144,24]{1,0:T(8,128)(2,1)} copy(bf16[144,24]{0,1:T(8,128)(2,1)} %param.6) | data formatting | bytes 13824 | tf_op args[1]
  1.4 137.2 %shard_map.55 = f32[24,3]{1,0:T(8,128)} custom-call(bf16[18,144,144,144]{3,2,1,0:T(8,128)(2,1)} %a_ref.1, bf16[144,24]{1,0:T(8,128)(2,1)} %copy.6.co_ref, bf16[144,120]{1,0:T(8,128)(2,1)} %cv_ref.1, f32[24]{0:T(128)} %eo_ref.1, f32[1,120]{1,0:T(1,128)} %bitcast.1), custom_call_target="tpu_custom_call" | custom-call | tf_op jit(solution)/shard_map/pallas_call | solution.py:279
  138.6 1.4 copy.7

commit v4 on v3

--- a/solution.py
+++ b/solution.py
@@ -17,7 +17,7 @@
 IC = 4
 CUT = 176
 PG = 4
-DEFER = 15
+DEFER = 16
 
 
 def iota(shape, dim):
@@ -28,13 +28,13 @@
     return (iota((n, n), 0) == iota((n, n), 1)).astype(BF16)
 
 
-def kernel(ndev, a_ref, co_ref, cv_ref, eo_ref, ev_ref, e_ref,
-           abuf, t_scr, h_scr, g_scr, recv_a, recv_b, v_sum, v_in, kron, kron_last, cot, cvt, cvp, evrow, es,
+def kernel(ndev, a_ref, cot, cv_ref, eo_ref, ev_ref, e_ref,
+           abuf, t_scr, h_scr, g_scr, recv_a, recv_b, v_sum, v_in, kron, kron_last, cvt, cvp, evrow, es,
            a_sem, send_sem, recv_sem, vsend_sem, vrecv_sem):
     rows_p, n = a_ref.shape[0], a_ref.shape[1]
-    o, v = co_ref.shape[1], cv_ref.shape[1]
+    o, v = cot.shape[0], cv_ref.shape[1]
     od = o // ndev
-    pts = od * v
+    pts = od * v - TILE
     nqb = n // QB
     me = lax.axis_index("dev")
     recv = (recv_a, recv_b)
@@ -61,14 +61,11 @@
     for k in range(1, 6):
         pl.semaphore_signal(barrier, inc=1, device_id={"dev": partner(k)}, device_id_type=MESH)
 
-    cot[...] = lax.dot_general(eye(o), co_ref[...], NT, preferred_element_type=F32).astype(BF16)
     cvt[...] = lax.dot_general(eye(v), cv_ref[...], NT, preferred_element_type=F32).astype(BF16)
     cvp[...] = jnp.zeros_like(cvp)
     cvp[:, :v] = cv_ref[...]
     evrow[...] = jnp.ones_like(evrow)
     evrow[:, :v] = ev_ref[...]
-
-    pl.semaphore_wait(barrier, 5)
 
     def send(h, s, t, p):
         k = slots(h)[s]
@@ -84,6 +81,24 @@
             src_ref=v_sum.at[(1,) + part], dst_ref=v_in.at[part],
             send_sem=vsend_sem.at[h, c], recv_sem=vrecv_sem.at[h, c],
             device_id={"dev": partner(second[h])}, device_id_type=MESH)
+
+    spare = LANES - v
+    lane = iota((TILE, LANES), 1)
+
+    def pack(blocks):
+        extra = blocks[-1][v - TILE:]
+        rows = jnp.concatenate(blocks, 0)[:pts]
+        moved = [jnp.where(lane < v, rows[m * TILE:(m + 1) * TILE], pltpu.roll(extra, v - m * spare, 1))
+                 for m in range(v // spare)]
+        return jnp.concatenate(moved + [rows[v // spare * TILE:]], 0)
+
+    def unpack(rows):
+        extra = jnp.zeros((TILE, LANES), F32)
+        for m in range(v // spare):
+            x = pltpu.roll(rows[m * TILE:(m + 1) * TILE], LANES - v + m * spare, 1)
+            extra = jnp.where((lane >= m * spare) & (lane < (m + 1) * spare), x, extra)
+        rows = jnp.where(iota(rows.shape, 1) < v, rows, 0.0)
+        return jnp.concatenate([rows, extra], 0)
 
     def make_kron():
         spread = (iota((o * TILE, o), 0) // TILE == iota((o * TILE, o), 1)).astype(BF16)
@@ -175,12 +190,12 @@
             for x in mine:
                 fetch((p + 1) % rows_p, x).start()
         second_step(CHUNKS - 1)
-        for j in range(0, o, 2):
-            h = jnp.concatenate([h_scr[pl.ds(j + x, n, stride=o), :] for x in range(2)], 1).astype(BF16)
-            g = jnp.dot(cvt[...], h, preferred_element_type=F32).astype(BF16)
+        for d in range(0, ndev, 2):
+            h = jnp.concatenate([h_scr[pl.ds(d * od + x, n, stride=o), :] for x in range(2 * od)], 1).astype(BF16)
+            g = jnp.dot(cvt[...], h, preferred_element_type=F32)
+            g = [g[:, x * LANES:(x + 1) * LANES] for x in range(2 * od)]
             for x in range(2):
-                d, r = divmod(j + x, od)
-                g_scr[p, d, r * v:(r + 1) * v, :] = g[:, x * LANES:(x + 1) * LANES]
+                g_scr[p, d + x] = pack(g[x * od:(x + 1) * od]).astype(BF16)
         for s in (2, 3, 1):
             for h in range(2):
                 send(h, s, 1, p).start()
@@ -189,43 +204,34 @@
         def _():
             late(p, 0)
 
-        @pl.when(p == 0)
-        def _():
-            make_kron()
-            v_sum[...] = jnp.zeros_like(v_sum)
-
-        @pl.when((p % PG == PG - 1) & (p > PG))
+        @pl.when((p % PG == 1) & (p > PG))
         def _():
             g = p // PG - 1
-
-            def target(t, _):
-                group(t, g, g * PG, PG)
-                return 0
-
-            lax.fori_loop(0, 2, target, 0)
-        return 0
-
+            group(1, g, g * PG, PG)
+        return 0
+
+    make_kron()
+    v_sum[...] = jnp.zeros_like(v_sum)
+    pl.semaphore_wait(barrier, 5)
     lax.fori_loop(0, rows_p, row, 0)
     lax.fori_loop(DEFER, rows_p, late, 0)
     groups = rows_p // PG
-
-    def finish(u, _):
-        group(1 - u, groups - 1, (groups - 1) * PG, PG)
-        group(1 - u, groups, groups * PG, rows_p % PG)
-
-        @pl.when(u == 0)
-        def _():
-            def start_sum(c, _):
-                for h in range(2):
-                    send_sum(h, c).start()
-                return 0
-
-            lax.fori_loop(0, o // IC, start_sum, 0)
-        return 0
-
-    lax.fori_loop(0, 2, finish, 0)
-
-    v_in[:, pts:, :] = jnp.zeros_like(v_in[:, pts:, :])
+    group(1, groups, groups * PG, rows_p % PG)
+
+    def start_sum(c, _):
+        for h in range(2):
+            send_sum(h, c).start()
+        return 0
+
+    lax.fori_loop(0, o // IC, start_sum, 0)
+
+    def own(g, _):
+        group(0, g, g * PG, PG)
+        return 0
+
+    lax.fori_loop(0, groups, own, 0)
+    group(0, groups, groups * PG, rows_p % PG)
+
     evb = jnp.broadcast_to(evrow[...], (LANES, LANES))
     evsum = (evb + evb.T)[:v]
 
@@ -235,11 +241,10 @@
 
         def one(x, _):
             i = c * IC + x
+            full = unpack(v_sum[0, i] + v_in[i])
             for j in range(od):
-                at = pl.ds(j * v, LANES)
-                x = v_sum[0, i, at, :] + v_in[i, at, :]
-                xt = x.T[:v]
-                x = x[:v]
+                x = full[j * v:(j + 1) * v]
+                xt = jnp.concatenate([x, jnp.zeros((spare, LANES), F32)], 0).T[:v]
                 e = x * (2.0 * x - xt) / (eo_ref[me * od + j] + eo_ref[i] - evsum)
                 es[j, i] = jnp.sum(e.reshape(v // 8, 8, LANES), 0)
             return 0
@@ -274,7 +279,7 @@
         rows_p, n = a_ints.shape[:2]
         o, v = c_occ.shape[1], c_vir.shape[1]
         od = o // ndev
-        pts = od * v
+        pts = od * v - TILE
         vm = pl.BlockSpec(memory_space=pltpu.VMEM)
         return pl.pallas_call(
             functools.partial(kernel, ndev),
@@ -288,11 +293,10 @@
                 pltpu.VMEM((rows_p, ndev, pts, LANES), BF16),
                 pltpu.VMEM((3, rows_p, 2, CUT, LANES), BF16),
                 pltpu.VMEM((3, rows_p, 2, pts - CUT, LANES), BF16),
-                pltpu.VMEM((2, o, pts + 8, LANES), F32),
-                pltpu.VMEM((o, pts + 8, LANES), F32),
+                pltpu.VMEM((2, o, pts, LANES), F32),
+                pltpu.VMEM((o, pts, LANES), F32),
                 pltpu.VMEM((2, 4, o * TILE, 16 * TILE), BF16),
                 pltpu.VMEM((2, o * TILE, 8 * TILE), BF16),
-                pltpu.VMEM((o, n), BF16),
                 pltpu.VMEM((v, n), BF16),
                 pltpu.VMEM((n, LANES), BF16),
                 pltpu.VMEM((1, LANES), F32),
@@ -305,7 +309,7 @@
             ],
             compiler_params=pltpu.CompilerParams(
                 collective_id=0, has_side_effects=True, vmem_limit_bytes=62 * 2**20),
-        )(a_ints, c_occ, c_vir, eps_occ, eps_vir.reshape(1, v))
+        )(a_ints, c_occ.T, c_vir, eps_occ, eps_vir.reshape(1, v))
 
     return jax.shard_map(
         per_device,

time: 140 us -> 134 us (0.957)
  Pallas kernels: 137 us -> 132 us
  local copies, waits for them, and re-layouts: 2.77 us -> 1.36 us
    pallas_call x1, Pallas kernels: 137 us -> 132 us  [per_device(): pl.pallas_call(functools.partial(kernel, ndev), out_shape=jax.ShapeDtypeS...]
    unnamed x1 -> x0, local copies, waits for them, and re-layouts: 1.41 us -> none
where the time goes in v4:
time: 134 us
  Pallas kernels  132 us (99%)
  local copies, waits for them, and re-layouts  1.36 us (1%)
    pallas_call x1, Pallas kernels, per_device(): pl.pallas_call(functools.partial(kernel, ndev), out_shape=jax.ShapeDtypeS...  132 us

profile of v4, /device:TPU:0, one launch (start us, length us, event | category | flops | bytes accessed | tf_op | source)
XLA Modules:
  0.0 133.8 jit_solution(3454342098654216387)
XLA Ops:
  0.0 132.4 %shard_map.55 = f32[24,3]{1,0:T(8,128)} custom-call(bf16[18,144,144,144]{3,2,1,0:T(8,128)(2,1)} %a_ref.1, bf16[24,144]{1,0:T(8,128)(2,1)} %bitcast.2, bf16[144,120]{1,0:T(8,128)(2,1)} %cv_ref.1, f32[24]{0:T(128)} %eo_ref.1, f32[1,120]{1,0:T(1,128)} %bitcast.3), custom_call_target="tpu_custom_call" | custom-call | tf_op jit(solution)/shard_map/pallas_call | solution.py:284
  132.4 1.4 %copy.6 = f32[24,3]{0,1:T(4,128)} copy(f32[24,3]{1,0:T(8,128)} %shard_map.55) | data formatting | bytes 576 | tf_op jit(solution)/shard_map/pallas_call | solution.py:284

commit v5 on v4

--- a/solution.py
+++ b/solution.py
@@ -193,9 +193,10 @@
         for d in range(0, ndev, 2):
             h = jnp.concatenate([h_scr[pl.ds(d * od + x, n, stride=o), :] for x in range(2 * od)], 1).astype(BF16)
             g = jnp.dot(cvt[...], h, preferred_element_type=F32)
+            g = g.astype(BF16)
             g = [g[:, x * LANES:(x + 1) * LANES] for x in range(2 * od)]
             for x in range(2):
-                g_scr[p, d + x] = pack(g[x * od:(x + 1) * od]).astype(BF16)
+                g_scr[p, d + x] = pack(g[x * od:(x + 1) * od])
         for s in (2, 3, 1):
             for h in range(2):
                 send(h, s, 1, p).start()
@@ -249,7 +250,7 @@
                 es[j, i] = jnp.sum(e.reshape(v // 8, 8, LANES), 0)
             return 0
 
-        lax.fori_loop(0, IC, one, 0)
+        lax.fori_loop(0, IC, one, 0, unroll=True)
         return 0
 
     lax.fori_loop(0, o // IC, energies, 0)

time: 134 us -> 133 us (level)
  no operation moved by 1% of the time
where the time goes in v5:
time: 133 us
  Pallas kernels  132 us (99%)
  local copies, waits for them, and re-layouts  1.36 us (1%)
    pallas_call x1, Pallas kernels, per_device(): pl.pallas_call(functools.partial(kernel, ndev), out_shape=jax.ShapeDtypeS...  132 us

profile of v5, /device:TPU:0, one launch (start us, length us, event | category | flops | bytes accessed | tf_op | source)
XLA Modules:
  0.0 133.2 jit_solution(15978861753668764377)
XLA Ops:
  0.0 131.9 %shard_map.55 = f32[24,3]{1,0:T(8,128)} custom-call(bf16[18,144,144,144]{3,2,1,0:T(8,128)(2,1)} %a_ref.1, bf16[24,144]{1,0:T(8,128)(2,1)} %bitcast.2, bf16[144,120]{1,0:T(8,128)(2,1)} %cv_ref.1, f32[24]{0:T(128)} %eo_ref.1, f32[1,120]{1,0:T(1,128)} %bitcast.3), custom_call_target="tpu_custom_call" | custom-call | tf_op jit(solution)/shard_map/pallas_call | solution.py:285
  131.9 1.4 %copy.6 = f32[24,3]{0,1:T(4,128)} copy(f32[24,3]{1,0:T(8,128)} %shard_map.55) | data formatting | bytes 576 | tf_op jit(solution)/shard_map/pallas_call | solution.py:285
